TPU v7x, 128 devices: a whole 4x4x4 slice. The times are simulated.
128 devices in a mesh: inst: 8 (over y_hi, x), head: 16 (over y_lo, z, core).
Axes of the slice: x: 4, y: 4 (y_hi: 2, y_lo: 2; y = y_hi * 2 + y_lo), z: 4, core: 2. Of those that a mesh axis runs over, the one named last changes fastest.
Arguments:
- old_keys: bfloat16 [1024, 16, 64, 128], P('inst', 'head'), may hold values from -6 to 6
- old_values: bfloat16 [1024, 16, 64, 128], P('inst', 'head'), may hold values from -6 to 6
- old_block: int32 [1024], P('inst'), may hold values from -1 to 255, as said below
- new_slot: int32 [256], replicated, may hold values from 0 to 255, as said below
- lengths: int32 [64], replicated, may hold values from 1 to 16384, as said below
- queries: bfloat16 [64, 16, 8192], P(None, None, 'head'), may hold values from -240 to 240
- draft_keys: bfloat16 [64, 16, 1024], P('inst'), may hold values from -6 to 6
- draft_values: bfloat16 [64, 16, 1024], P('inst'), may hold values from -6 to 6
Outputs:
- moved_keys: bfloat16 [256, 16, 64, 128], P('inst', 'head')
- moved_values: bfloat16 [256, 16, 64, 128], P('inst', 'head')
- attended: bfloat16 [64, 16, 8192], P(None, None, 'head')
Inputs may be any that keep to these rules, and one draw needn't show every extreme that they name: ceil(lengths / 128) summed over the requests is exactly 256; the longest request has exactly 16384 tokens. `old_block`: every block 0 to 255 stands in exactly one old slot; the blocks fill all slots of 2 instances and all other slots hold -1. A permutation; block g goes to instance new_slot[g] // 32. At most 32 blocks go from one old instance to one new one, and in every draw some new instance receives all its 32 blocks from a single old instance.
All inputs are finite; a program needn't handle non-finite values.
Results may differ from a plain program's by a relative error of at most 0.004.
Values may be sent and summed in bfloat16 or wider, within the bound.
No kernel may reach another device: no remote copies, remote signals or barrier semaphores. Data moves between devices by JAX's collectives and lax.ppermute only.
A program may use at most 64 MiB of HBM per device.

v0:
```python
import math

import jax
import jax.numpy as jnp
from jax import lax
from jax.sharding import PartitionSpec as P

BLK = 128
DRAFT = 16


masked = -1e30


def partner(block, axis, stride):
    count = lax.axis_size(axis)
    route = []
    for low in range(count):
        high = low | 1 << stride
        if high != low and high < count:
            route += [(low, high), (high, low)]
    return lax.ppermute(block, axis, route)


def sent_to_all(shard, axis):
    devices = lax.axis_size(axis)
    return lax.all_to_all(
        jnp.broadcast_to(shard[None], (devices, *shard.shape)), axis, 0, 0, tiled=True
    )


def taken_together(shard, axis):
    return sent_to_all(shard, axis).max(axis=0)


def join_partials(earlier, later):
    raised = jnp.maximum(earlier[0], later[0])
    keep_early = jnp.exp(earlier[0] - raised)
    keep_late = jnp.exp(later[0] - raised)
    totals = earlier[1] * keep_early + later[1] * keep_late
    weighted = earlier[2] * keep_early[..., None] + later[2] * keep_late[..., None]
    return (raised, totals, weighted)


def cache_partial(key_cache, value_cache, block_list, lengths, grouped, head_base):
    slot_count, entries, half_len, head_dim = key_cache.shape
    requests, qcount, _ = grouped.shape
    inv_root = 1.0 / math.sqrt(head_dim)
    counts = (lengths + BLK - 1) // BLK
    starts = jnp.cumsum(counts) - counts
    filled = block_list >= 0
    block_owner_list = (
        jnp.sum((starts[None, :] <= block_list[:, None]).astype(jnp.int32), axis=1) - 1
    )
    block_owner_list = jnp.clip(block_owner_list, 0, requests - 1)
    offset = block_list - starts[block_owner_list]
    halves = (head_base + jnp.arange(entries, dtype=jnp.int32)) % 2
    within = (halves[:, None] * half_len + jnp.arange(half_len, dtype=jnp.int32)[None, :]).reshape(
        entries * half_len
    )
    positions = offset[:, None] * BLK + within[None, :]
    usable = filled[:, None] & (positions < lengths[block_owner_list][:, None])
    stride = math.gcd(slot_count, 64)
    nsteps = slot_count // stride
    token_count = entries * half_len
    key_rows_all = key_cache.reshape(nsteps, stride, token_count, head_dim)
    value_rows_all = value_cache.reshape(nsteps, stride, token_count, head_dim)
    request_ids = jnp.arange(requests, dtype=jnp.int32)

    def advance(state_now, pieces):
        peaks, totals, weighted = state_now
        key_rows, value_rows, rows_owner, rows_filled, rows_usable = pieces
        picked = grouped[rows_owner]
        scores = (
            jnp.einsum("sqd,std->sqt", picked, key_rows, preferred_element_type=jnp.float32)
            * inv_root
        )
        scores = jnp.where(rows_usable[:, None, :], scores, masked)
        belongs = (rows_owner[:, None] == request_ids[None, :]) & rows_filled[:, None]
        slot_peaks = jnp.max(scores, axis=-1)
        block_peak = jnp.max(jnp.where(belongs[:, :, None], slot_peaks[:, None, :], masked), axis=0)
        raised = jnp.maximum(peaks, block_peak)
        weights = jnp.where(
            rows_usable[:, None, :], jnp.exp(scores - raised[rows_owner][:, :, None]), 0.0
        )
        belongs_f = belongs.astype(jnp.float32)
        row_sums = jnp.dot(
            belongs_f.T,
            jnp.sum(weights, axis=-1),
            precision=lax.Precision.HIGHEST,
            preferred_element_type=jnp.float32,
        )
        blended = jnp.einsum(
            "sqt,std->sqd",
            weights.astype(jnp.bfloat16),
            value_rows,
            preferred_element_type=jnp.float32,
        )
        gathered = jnp.einsum("sr,sqd->rqd", belongs_f, blended, precision=lax.Precision.HIGHEST)
        rescale = jnp.exp(peaks - raised)
        return (
            (raised, totals * rescale + row_sums, weighted * rescale[..., None] + gathered),
            None,
        )

    start_state = (
        jnp.full((requests, qcount), masked, jnp.float32),
        jnp.zeros((requests, qcount), jnp.float32),
        jnp.zeros((requests, qcount, head_dim), jnp.float32),
    )
    pieces = (
        key_rows_all,
        value_rows_all,
        block_owner_list.reshape(nsteps, stride),
        filled.reshape(nsteps, stride),
        usable.reshape(nsteps, stride, token_count),
    )
    return lax.scan(advance, start_state, pieces)[0]


def draft_partial(grouped, draft_keys, draft_values, current_replica, head_base):
    requests, qcount, head_dim = grouped.shape
    per_token = qcount // DRAFT
    rows_loc = draft_keys.shape[0]
    kv_head = head_base // 2
    own_keys = lax.dynamic_slice_in_dim(draft_keys, kv_head * head_dim, head_dim, 2)
    own_vals = lax.dynamic_slice_in_dim(draft_values, kv_head * head_dim, head_dim, 2)
    own_q = lax.dynamic_slice_in_dim(grouped, current_replica * rows_loc, rows_loc, 0).reshape(
        rows_loc, DRAFT, per_token, head_dim
    )
    inv_root = 1.0 / math.sqrt(head_dim)
    scores = (
        jnp.einsum("rigd,rjd->rigj", own_q, own_keys, preferred_element_type=jnp.float32) * inv_root
    )
    causal = jnp.arange(DRAFT)[None, :] <= jnp.arange(DRAFT)[:, None]
    causal_flat = jnp.broadcast_to(causal[:, None, :], (DRAFT, per_token, DRAFT)).reshape(
        qcount, DRAFT
    )
    scores = jnp.where(causal_flat, scores.reshape(rows_loc, qcount, DRAFT), masked)
    peaks = jnp.max(scores, axis=-1)
    weights = jnp.where(causal_flat, jnp.exp(scores - peaks[..., None]), 0.0)
    totals = jnp.sum(weights, axis=-1)
    weighted = jnp.einsum(
        "rqj,rjd->rqd", weights.astype(jnp.bfloat16), own_vals, preferred_element_type=jnp.float32
    )
    include = head_base % 2 == 0
    peaks = jnp.where(include, peaks, masked)
    totals = jnp.where(include, totals, 0.0)
    weighted = jnp.where(include, weighted, 0.0)
    first_row = current_replica * rows_loc
    full_peaks = lax.dynamic_update_slice_in_dim(
        jnp.full((requests, qcount), masked, jnp.float32), peaks, first_row, 0
    )
    full_totals = lax.dynamic_update_slice_in_dim(
        jnp.zeros((requests, qcount), jnp.float32), totals, first_row, 0
    )
    full_weighted = lax.dynamic_update_slice_in_dim(
        jnp.zeros((requests, qcount, head_dim), jnp.float32), weighted, first_row, 0
    )
    return (full_peaks, full_totals, full_weighted)


def shards(old_keys, old_values, old_block, new_slot, lengths, queries, draft_keys, draft_values):
    replica_count = lax.axis_size("inst")
    current_replica = lax.axis_index("inst")
    me_head = lax.axis_index("head")
    entries = old_keys.shape[1]
    head_dim = old_keys.shape[3]
    head_base = me_head * entries
    block_capacity = new_slot.shape[0]
    slots_per_replica = block_capacity // replica_count
    destination_replica = jnp.where(
        old_block >= 0, new_slot[jnp.clip(old_block, 0, block_capacity - 1)], block_capacity
    )
    trailing_tokens = old_keys.shape[1:]
    outgoing_keys = (
        jnp.zeros((block_capacity,) + trailing_tokens, old_keys.dtype)
        .at[destination_replica]
        .set(old_keys, mode="drop")
    )
    outgoing_values = (
        jnp.zeros((block_capacity,) + trailing_tokens, old_values.dtype)
        .at[destination_replica]
        .set(old_values, mode="drop")
    )
    outgoing_keys = outgoing_keys.reshape((replica_count, slots_per_replica) + trailing_tokens)
    outgoing_values = outgoing_values.reshape((replica_count, slots_per_replica) + trailing_tokens)
    inbox_k, inbox_v = (
        lax.all_to_all(outgoing_keys, "inst", split_axis=0, concat_axis=0, tiled=True),
        lax.all_to_all(outgoing_values, "inst", split_axis=0, concat_axis=0, tiled=True),
    )
    moved_keys = jnp.sum(inbox_k, axis=0)
    moved_values = jnp.sum(inbox_v, axis=0)
    local_heads = queries.shape[2] // head_dim
    requests = queries.shape[0]
    locally_present = (
        jnp.zeros((block_capacity,), jnp.int32)
        .at[new_slot]
        .set(jnp.arange(block_capacity, dtype=jnp.int32))
    )
    key_cache = moved_keys
    value_cache = moved_values
    block_list = lax.dynamic_slice_in_dim(
        locally_present, current_replica * slots_per_replica, slots_per_replica
    )
    split_tokens = False
    is_lower = me_head % 2 == 0
    other_k, other_v = partner((key_cache, value_cache), "head", 0)
    key_cache = jnp.where(
        is_lower,
        jnp.concatenate([key_cache, other_k], axis=1),
        jnp.concatenate([other_k, key_cache], axis=1),
    )
    value_cache = jnp.where(
        is_lower,
        jnp.concatenate([value_cache, other_v], axis=1),
        jnp.concatenate([other_v, value_cache], axis=1),
    )
    head_base = me_head - me_head % 2
    grouped = queries
    qcount = grouped.shape[2] // head_dim
    grouped = grouped.reshape(requests, DRAFT * qcount, head_dim)
    cached = cache_partial(key_cache, value_cache, block_list, lengths, grouped, head_base)
    drafted = draft_partial(grouped, draft_keys, draft_values, current_replica, head_base)
    peaks, totals, weighted = join_partials(cached, drafted)
    peaks = peaks.reshape(requests, DRAFT, local_heads)
    totals = totals.reshape(requests, DRAFT, local_heads)
    weighted = weighted.reshape(requests, DRAFT, local_heads, head_dim)
    top_score = taken_together(peaks, "inst")
    factor = jnp.exp(peaks - top_score)
    totals, weighted = lax.psum((totals * factor, weighted * factor[..., None]), "inst")
    attended = (
        (weighted / totals[..., None])
        .astype(jnp.bfloat16)
        .reshape(requests, DRAFT, local_heads * head_dim)
    )
    return (moved_keys, moved_values, attended)


def solution(mesh):
    placed = (
        P("inst", "head", None, None),
        P("inst", "head", None, None),
        P("inst"),
        P(),
        P(),
        P(None, None, "head"),
        P("inst", None, None),
        P("inst", None, None),
    )
    return jax.shard_map(
        shards,
        mesh=mesh,
        in_specs=placed,
        out_specs=(
            P("inst", "head", None, None),
            P("inst", "head", None, None),
            P(None, None, "head"),
        ),
        check_vma=False,
    )
```

profile of v0, /device:TPU:0, one launch (start us, length us, event | category | flops | bytes accessed | tf_op | source)
XLA Modules:
  0.0 294.1 jit_solution(11643175703798855728)
XLA Ops:
  7.2 0.7 compare_select_fusion.3
  7.9 1.6 gather_fusion
  9.5 0.7 compare_select_fusion.2
  10.2 3.0 %broadcast.234.clone = bf16[256,64,128]{2,1,0:T(8,128)(2,1)} broadcast(bf16[]{:T(256)} %constant.110.clone.1), dimensions={} | broadcast | bytes 4194306 | tf_op jit(solution)/shard_map/broadcast.25
  13.2 14.2 %scatter_fusion = bf16[256,64,128]{2,1,0:T(8,128)(2,1)} fusion(bf16[256,64,128]{2,1,0:T(8,128)(2,1)} %broadcast.234.clone, s32[128]{0:T(128)S(1)} %compare_select_fusion.2, bf16[128,64,128]{2,1,0:T(8,128)(2,1)S(1)} %bitcast.45), kind=kCustom, calls=%fused_computation.5 | custom fusion | bytes 6291968 | tf_op jit(solution)/shard_map/scatter | solution.py:179
  27.4 7.1 %all-to-all-start = ((bf16[8,32,1,64,128]{4,3,1,2,0:T(8,128)(2,1)}), bf16[8,32,1,64,128]{4,3,1,2,0:T(8,128)(2,1)}, u32[]{:S(2)}, u32[]{:S(2)}) async-start(bf16[8,32,1,64,128]{4,3,1,2,0:T(8,128)(2,1)} %bitcast.41), calls=%async_computation | async-start | bytes 8388608 | tf_op jit(solution)/shard_map/all_to_all | solution.py:189
  34.5 3.0 %broadcast.234.clone.1 = bf16[256,64,128]{2,1,0:T(8,128)(2,1)} broadcast(bf16[]{:T(256)} %constant.110.clone.1), dimensions={} | broadcast | bytes 4194306 | tf_op jit(solution)/shard_map/broadcast.25
  37.5 14.2 %scatter_fusion.1 = bf16[256,64,128]{2,1,0:T(8,128)(2,1)} fusion(bf16[256,64,128]{2,1,0:T(8,128)(2,1)} %broadcast.234.clone.1, s32[128]{0:T(128)S(1)} %compare_select_fusion.2, bf16[128,64,128]{2,1,0:T(8,128)(2,1)S(1)} %bitcast.46), kind=kCustom, calls=%fused_computation.6 | custom fusion | bytes 6291968 | tf_op jit(solution)/shard_map/scatter | solution.py:184
  51.7 33.7 %all-to-all-done = bf16[8,32,1,64,128]{4,3,1,2,0:T(8,128)(2,1)} async-done(((bf16[8,32,1,64,128]{4,3,1,2,0:T(8,128)(2,1)}), bf16[8,32,1,64,128]{4,3,1,2,0:T(8,128)(2,1)}, u32[]{:S(2)}, u32[]{:S(2)}) %all-to-all-start) | async-done | bytes 4194336 | tf_op jit(solution)/shard_map/all_to_all | solution.py:189
  85.5 17.3 %all-to-all-start.1 = ((bf16[8,32,1,64,128]{4,3,1,2,0:T(8,128)(2,1)}), bf16[8,32,1,64,128]{4,3,1,2,0:T(8,128)(2,1)}, u32[]{:S(2)}, u32[]{:S(2)}) async-start(bf16[8,32,1,64,128]{4,3,1,2,0:T(8,128)(2,1)} %bitcast.40), calls=%async_computation.1 | async-start | bytes 8388608 | tf_op jit(solution)/shard_map/all_to_all | solution.py:190
  103.1 1.4 scatter_custom_fusion.2
  104.8 0.7 gather_fusion.2
  105.5 0.7 gather_fusion.1
  106.2 0.7 reshape.240
  107.0 1.2 select_reduce_fusion.2
  109.0 3.1 %reduce_sum.56 = bf16[32,64,128]{2,1,0:T(8,128)(2,1)S(1)} reduce(bf16[8,32,1,64,128]{4,3,1,2,0:T(8,128)(2,1)} %all-to-all-done, bf16[]{:T(256)} %constant.110.clone.1), dimensions={0,2}, to_apply=%region_1.2 | reduce | flops 1835008 | bytes 4718594 | tf_op jit(solution)/shard_map/reduce_sum | solution.py:192
  112.2 0.7 broadcast.223
  112.9 0.6 constant_dynamic-update-slice_fusion
  113.8 0.7 gather_fusion.3
  114.7 0.2 fusion.13
  115.0 1.6 broadcast.233
  116.6 0.9 fusion.11
  117.5 35.1 %all-to-all-done.1 = bf16[8,32,1,64,128]{4,3,1,2,0:T(8,128)(2,1)} async-done(((bf16[8,32,1,64,128]{4,3,1,2,0:T(8,128)(2,1)}), bf16[8,32,1,64,128]{4,3,1,2,0:T(8,128)(2,1)}, u32[]{:S(2)}, u32[]{:S(2)}) %all-to-all-start.1) | async-done | bytes 4194336 | tf_op jit(solution)/shard_map/all_to_all | solution.py:190
  152.6 3.1 %reduce_sum.58 = bf16[32,64,128]{2,1,0:T(8,128)(2,1)S(1)} reduce(bf16[8,32,1,64,128]{4,3,1,2,0:T(8,128)(2,1)} %all-to-all-done.1, bf16[]{:T(256)} %constant.110.clone.1), dimensions={0,2}, to_apply=%region_3.4 | reduce | flops 1835008 | bytes 4718594 | tf_op jit(solution)/shard_map/reduce_sum | solution.py:193
  155.9 0.9 fusion.37
  156.8 0.3 select_reduce_fusion
  157.2 0.6 gather_fusion.4
  157.8 0.7 fusion.4
  158.5 1.3 maximum_select_fusion.1
  159.8 0.5 fusion.6
  160.3 0.7 copy.134
  161.0 0.7 copy.127
  161.7 0.7 copy.121
  162.5 0.6 copy-done.8
  163.1 0.8 reshape.327
  163.9 13.6 %all-to-all-start.2 = ((f32[8,1,4096]{2,1,0:T(1,128)}), f32[8,1,4096]{2,1,0:T(1,128)S(1)}, u32[]{:S(2)}, u32[]{:S(2)}) async-start(f32[8,1,4096]{2,1,0:T(1,128)} %reshape.327), calls=%async_computation.2 | async-start | bytes 262144 | tf_op jit(solution)/shard_map/all_to_all | solution.py:27
  177.8 4.6 %multiply_add_fusion = f32[64,64,128]{2,0,1:T(8,128)S(1)} fusion(f32[64,64,128]{2,0,1:T(8,128)} %fusion.11, f32[32,64,128]{2,1,0:T(8,128)S(1)} %fusion.6, f32[64,64]{0,1:T(8,128)} %copy.134, f32[64,64]{0,1:T(8,128)} %copy.127, f32[64,64]{0,1:T(8,128)} %copy.121, s32[32]{0:T(128)} %copy-done.17, pred[32]{0:T(512)(128)(4,1)} %copy-done.15), kind=kOutput, calls=%fused_computation.9 | convolution fusion | flops 203427840 | bytes 5292192 | tf_op jit(solution)/shard_map/while/body/eval_jaxpr/sr,sqd->rqd/dot_general | solution.py:99
  182.4 1.1 fusion.2
  183.6 2.0 all-to-all-done.2
  185.6 0.5 broadcast.293
  186.1 1.0 reduce.7
  187.2 0.8 copy_multiply_fusion
  188.0 1.9 broadcast_multiply_fusion
  189.9 40.0 %psum.15 = f32[64,16,4]{0,1,2:T(8,128)S(1)} all-reduce(f32[64,16,4]{0,1,2:T(8,128)S(1)} %get-tuple-element.25), channel_id=1, replica_groups=mesh['inst'=8,'head'=16] {'inst'}, use_global_device_ids=true, to_apply=%region_14.15 | all-reduce | flops 4096 | bytes 32768 | tf_op jit(solution)/shard_map/psum | solution.py:231
  229.9 53.4 %all-reduce.2.cloned.1.call-done = f32[64,16,4,128]{3,0,2,1:T(8,128)} async-done(((f32[64,16,4,128]{3,0,2,1:T(8,128)}), f32[64,16,4,128]{3,0,2,1:T(8,128)}) %all-reduce.2.cloned.1.call-update) | async-done | bytes 2097168 | tf_op jit(solution)/shard_map/psum | solution.py:231
  283.3 1.9 divide_convert_fusion
  285.2 0.8 copy.144
  286.1 1.2 reshape.247
  (87 shorter events, 2.9 us)
Async XLA Ops:
  7.2 107.5 %copy-start = (bf16[8,16,1024]{2,1,0:T(8,128)(2,1)S(1)}, bf16[8,16,1024]{2,1,0:T(8,128)(2,1)}, u32[]{:S(2)}) copy-start(bf16[8,16,1024]{2,1,0:T(8,128)(2,1)} %param.15) | copy-start | bytes 786436
  10.2 3.0 %copy-start.3 = (bf16[128,1,64,128]{3,2,1,0:T(8,128)(2,1)S(1)}, bf16[128,1,64,128]{3,2,1,0:T(8,128)(2,1)}, u32[]{:S(2)}) copy-start(bf16[128,1,64,128]{3,2,1,0:T(8,128)(2,1)} %param.8) | copy-start | bytes 6291460
  27.4 58.1 %all-to-all-start = ((bf16[8,32,1,64,128]{4,3,1,2,0:T(8,128)(2,1)}), bf16[8,32,1,64,128]{4,3,1,2,0:T(8,128)(2,1)}, u32[]{:S(2)}, u32[]{:S(2)}) async-start(bf16[8,32,1,64,128]{4,3,1,2,0:T(8,128)(2,1)} %bitcast.41), calls=%async_computation | async-start | bytes 8388608 | tf_op jit(solution)/shard_map/all_to_all | solution.py:189
  34.5 3.0 %copy-start.4 = (bf16[128,1,64,128]{3,2,1,0:T(8,128)(2,1)S(1)}, bf16[128,1,64,128]{3,2,1,0:T(8,128)(2,1)}, u32[]{:S(2)}) copy-start(bf16[128,1,64,128]{3,2,1,0:T(8,128)(2,1)} %param.9) | copy-start | bytes 6291460
  37.5 14.2 %copy-start.2 = (s32[256]{0:T(256)S(1)}, s32[256]{0:T(256)}, u32[]{:S(2)}) copy-start(s32[256]{0:T(256)} %param.11) | copy-start | bytes 3076
  85.5 17.3 %copy-start.1 = (s32[64]{0:T(128)S(1)}, s32[64]{0:T(128)}, u32[]{:S(2)}) copy-start(s32[64]{0:T(128)} %param.12) | copy-start | bytes 772
  85.5 20.8 %copy-start.7 = (bf16[64,16,512]{2,1,0:T(8,128)(2,1)S(1)}, bf16[64,16,512]{2,1,0:T(8,128)(2,1)}, u32[]{:S(2)}) copy-start(bf16[64,16,512]{2,1,0:T(8,128)(2,1)} %param.13) | copy-start | bytes 3145732
  85.5 67.1 %all-to-all-start.1 = ((bf16[8,32,1,64,128]{4,3,1,2,0:T(8,128)(2,1)}), bf16[8,32,1,64,128]{4,3,1,2,0:T(8,128)(2,1)}, u32[]{:S(2)}, u32[]{:S(2)}) async-start(bf16[8,32,1,64,128]{4,3,1,2,0:T(8,128)(2,1)} %bitcast.40), calls=%async_computation.1 | async-start | bytes 8388608 | tf_op jit(solution)/shard_map/all_to_all | solution.py:190
  104.6 4.3 %copy-start.15 = (pred[32]{0:T(512)(128)(4,1)}, pred[32]{0:T(512)(128)(4,1)S(1)}, u32[]{:S(2)}) copy-start(pred[32]{0:T(512)(128)(4,1)S(1)} %get-tuple-element.27) | copy-start | bytes 100
  108.8 3.3 %copy-start.17 = (s32[32]{0:T(128)}, s32[32]{0:T(128)S(1)}, u32[]{:S(2)}) copy-start(s32[32]{0:T(128)S(1)} %add_clamp_fusion) | copy-start | bytes 388
  112.1 43.7 %copy-start.5 = (bf16[32,64,128]{2,1,0:T(8,128)(2,1)}, bf16[32,64,128]{2,1,0:T(8,128)(2,1)S(1)}, u32[]{:S(2)}) copy-start(bf16[32,64,128]{2,1,0:T(8,128)(2,1)S(1)} %reduce_sum.56) | copy-start | bytes 1572868
  112.1 43.7 %collective-permute-start = (bf16[32,1,64,128]{3,2,1,0:T(8,128)(2,1)S(1)}, bf16[32,1,64,128]{3,2,1,0:T(8,128)(2,1)S(1)}, u32[]{:S(2)}, u32[]{:S(2)}) collective-permute-start(bf16[32,1,64,128]{3,2,1,0:T(8,128)(2,1)S(1)} %bitcast.47), channel_id=1, source_target_pairs={{0,1},{1,0},{2,3},{3,2},{4,5},{5,4},{6,7},{7,6},{8,9},{9,8},{10,11... | collective-permute-start | bytes 1572872 | tf_op jit(solution)/shard_map/ppermute | solution.py:22
  155.7 2.8 copy-start.6
  155.7 2.8 collective-permute-start.1
  157.2 2.7 copy-start.13
  157.2 3.1 %copy-start.11 = (f32[64,64]{1,0:T(8,128)}, f32[64,64]{1,0:T(8,128)S(1)}, u32[]{:S(2)}) copy-start(f32[64,64]{1,0:T(8,128)S(1)} %get-tuple-element.31) | copy-start | bytes 49156
  157.2 3.8 %copy-start.9 = (f32[64,64]{1,0:T(8,128)}, f32[64,64]{1,0:T(8,128)S(1)}, u32[]{:S(2)}) copy-start(f32[64,64]{1,0:T(8,128)S(1)} %get-tuple-element.30) | copy-start | bytes 49156
  162.5 0.6 copy-start.8
  163.9 21.6 %all-to-all-start.2 = ((f32[8,1,4096]{2,1,0:T(1,128)}), f32[8,1,4096]{2,1,0:T(1,128)S(1)}, u32[]{:S(2)}, u32[]{:S(2)}) async-start(f32[8,1,4096]{2,1,0:T(1,128)} %reshape.327), calls=%async_computation.2 | async-start | bytes 262144 | tf_op jit(solution)/shard_map/all_to_all | solution.py:27
  177.5 105.8 %all-reduce.2.cloned.1.call-start = ((), (), s32[]{:S(2)}) async-start(), calls=%async_computation.3 | async-start | bytes 4194304 | tf_op jit(solution)/shard_map/psum | solution.py:231
  177.7 4.7 %copy-start.10 = (f32[64,64]{1,0:T(8,128)S(1)}, f32[64,64]{1,0:T(8,128)}, u32[]{:S(2)}) copy-start(f32[64,64]{1,0:T(8,128)} %copy-done.9) | copy-start | bytes 49156
  177.7 4.7 %copy-start.12 = (f32[64,64]{1,0:T(8,128)S(1)}, f32[64,64]{1,0:T(8,128)}, u32[]{:S(2)}) copy-start(f32[64,64]{1,0:T(8,128)} %copy-done.11) | copy-start | bytes 49156
  177.7 4.7 %copy-start.14 = (f32[64,64]{1,0:T(8,128)S(1)}, f32[64,64]{1,0:T(8,128)}, u32[]{:S(2)}) copy-start(f32[64,64]{1,0:T(8,128)} %copy-done.13) | copy-start | bytes 49156
  177.7 4.7 %copy-start.16 = (pred[32]{0:T(512)(128)(4,1)S(1)}, pred[32]{0:T(512)(128)(4,1)}, u32[]{:S(2)}) copy-start(pred[32]{0:T(512)(128)(4,1)} %copy-done.15) | copy-start | bytes 100
  177.8 4.7 %copy-start.18 = (s32[32]{0:T(128)S(1)}, s32[32]{0:T(128)}, u32[]{:S(2)}) copy-start(s32[32]{0:T(128)} %copy-done.17) | copy-start | bytes 388
Sparse Core Ops, SparseCore 0:
  190.0 93.1 all-reduce.1
where the time goes:
time: 296 us; the launch traced here: 294 us
  waiting for transfers between devices  124 us (42%)
  local copies, waits for them, and re-layouts  51.1 us (17%)
  blocking collectives  40 us (14%)
  starting transfers between devices  38.3 us (13%)
  other arithmetic  17.4 us (6%)
  between operations  14.6 us (5%)
  matrix products  8.53 us (3%)
    psum x1, waiting for transfers between devices, shards(): lax.psum((totals * factor, weighted * factor[..., None]), 'inst')  53.4 us
    psum x1, blocking collectives, shards(): lax.psum((totals * factor, weighted * factor[..., None]), 'inst')  40 us
    all_to_all x1, waiting for transfers between devices, shards(): lax.all_to_all(outgoing_values, 'inst', split_axis=0, concat_axis=0, tile...  35.1 us
    all_to_all x1, waiting for transfers between devices, shards(): lax.all_to_all(outgoing_keys, 'inst', split_axis=0, concat_axis=0, tiled=...  33.7 us
    all_to_all x1, starting transfers between devices, shards(): lax.all_to_all(outgoing_values, 'inst', split_axis=0, concat_axis=0, tile...  17.3 us
    scatter x1, local copies, waits for them, and re-layouts, shards(): outgoing_keys = jnp.zeros((block_capacity,) + trailing_tokens, old_keys.d...  14.2 us
    scatter x1, local copies, waits for them, and re-layouts, shards(): outgoing_values = jnp.zeros((block_capacity,) + trailing_tokens, old_valu...  14.2 us
    all_to_all x1, starting transfers between devices, sent_to_all(): lax.all_to_all(jnp.broadcast_to(shard[None], (devices, *shard.shape)), ax...  13.6 us
  transfers between devices with their start and end apart: 6, of which 4 were waited for; matrix products, arithmetic and copies ran while one was open for 15% of the time, Pallas kernels for 0%

commit v1 on v0

v1 whole, which is shorter than its diff:
```python
import math

import jax
import jax.numpy as jnp
from jax import lax
from jax.experimental import pallas as pl
from jax.experimental.pallas import tpu as pltpu
from jax.sharding import PartitionSpec as P

BLK = 128
DRAFT = 16
masked = -1e30


def pack_body(old_block, new_slot, keys, values, out_k, out_v, zeros, owned, sem_k, sem_v):
    slots = keys.shape[0]
    total = out_k.shape[0]
    chunk = zeros.shape[0]
    zeros[...] = jnp.zeros(zeros.shape, zeros.dtype)
    is_source = old_block[0] >= 0

    @pl.when(is_source)
    def _():
        def clear(t, c):
            owned[t] = 0
            return c

        lax.fori_loop(0, total, clear, 0, unroll=8)

        def send(i, c):
            t = new_slot[jnp.maximum(old_block[i], 0)]
            owned[t] = 1
            pltpu.make_async_copy(keys.at[i], out_k.at[t], sem_k).start()
            pltpu.make_async_copy(values.at[i], out_v.at[t], sem_v).start()
            return c

        lax.fori_loop(0, slots, send, 0)

        def fill(t, c):
            @pl.when(owned[t] == 0)
            def _():
                pltpu.make_async_copy(zeros.at[0], out_k.at[t], sem_k).start()
                pltpu.make_async_copy(zeros.at[0], out_v.at[t], sem_v).start()

            return c

        lax.fori_loop(0, total, fill, 0)

    @pl.when(jnp.logical_not(is_source))
    def _():
        for j in range(total // chunk):
            pltpu.make_async_copy(zeros, out_k.at[pl.ds(j * chunk, chunk)], sem_k).start()
            pltpu.make_async_copy(zeros, out_v.at[pl.ds(j * chunk, chunk)], sem_v).start()

    pltpu.make_async_copy(out_k, out_k, sem_k).wait()
    pltpu.make_async_copy(out_v, out_v, sem_v).wait()


def pack(old_block, new_slot, keys, values):
    total = new_slot.shape[0]
    out = jax.ShapeDtypeStruct((total,) + keys.shape[1:], keys.dtype)
    anyspace = pl.BlockSpec(memory_space=pl.ANY)
    smem = pl.BlockSpec(memory_space=pltpu.SMEM)
    return pl.pallas_call(
        pack_body,
        in_specs=[smem, smem, anyspace, anyspace],
        out_specs=[anyspace, anyspace],
        out_shape=[out, out],
        scratch_shapes=[
            pltpu.VMEM((32,) + keys.shape[1:], keys.dtype),
            pltpu.SMEM((total,), jnp.int32),
            pltpu.SemaphoreType.DMA,
            pltpu.SemaphoreType.DMA,
        ],
        name="pack",
    )(old_block, new_slot, keys, values)


def split3(x):
    hi = lax.reduce_precision(x, 8, 7)
    rest = x - hi
    mid = lax.reduce_precision(rest, 8, 7)
    low = lax.reduce_precision(rest - mid, 8, 7)
    return jnp.stack([hi, mid, low], axis=1).astype(jnp.bfloat16)


def cache_partial(keys, values, old_block, lengths, grouped, me_head):
    other = [(i, i ^ 1) for i in range(lax.axis_size("head"))]
    other_k = lax.ppermute(keys, "head", other)
    other_v = lax.ppermute(values, "head", other)
    slots, half, head_dim = keys.shape
    requests, qcount, _ = grouped.shape
    inv_root = 1.0 / math.sqrt(head_dim)
    counts = (lengths + BLK - 1) // BLK
    starts = jnp.cumsum(counts) - counts
    filled = old_block >= 0
    owner = jnp.sum((starts[None, :] <= old_block[:, None]).astype(jnp.int32), axis=1) - 1
    owner = jnp.clip(owner, 0, requests - 1)
    owned = (owner[:, None] == jnp.arange(requests)[None, :]) & filled[:, None]
    offset = old_block - jnp.sum(jnp.where(owned, starts[None, :], 0), axis=1)
    limit = jnp.sum(jnp.where(owned, lengths[None, :], 0), axis=1)
    token = jnp.arange(2 * half, dtype=jnp.int32)
    within = jnp.where(me_head % 2 == 0, token, (token + half) % (2 * half))
    usable = filled[:, None] & (offset[:, None] * BLK + within[None, :] < limit[:, None])
    key_rows = jnp.concatenate([keys, other_k], axis=1)
    value_rows = jnp.concatenate([values, other_v], axis=1)
    picked = grouped[owner]
    scores = (
        jnp.einsum("sqd,std->sqt", picked, key_rows, preferred_element_type=jnp.float32) * inv_root
    )
    scores = jnp.where(usable[:, None, :], scores, masked)
    slot_peaks = jnp.max(scores, axis=-1)
    peaks = jnp.max(jnp.where(owned[:, :, None], slot_peaks[:, None, :], masked), axis=0)
    own_peak = jnp.max(jnp.where(owned[:, :, None], peaks[None], masked), axis=1)
    weights = jnp.where(usable[:, None, :], jnp.exp(scores - own_peak[:, :, None]), 0.0)
    owned_f = owned.astype(jnp.float32)
    totals = jnp.dot(
        owned_f.T,
        jnp.sum(weights, axis=-1),
        precision=lax.Precision.HIGHEST,
        preferred_element_type=jnp.float32,
    )
    blended = jnp.einsum(
        "sqt,std->sqd",
        weights.astype(jnp.bfloat16),
        value_rows,
        preferred_element_type=jnp.float32,
    )
    weighted = jnp.einsum("sr,sqd->rqd", owned_f, blended, precision=lax.Precision.HIGHEST)
    return peaks, totals, weighted


def draft_partial(grouped, draft_keys, draft_values, inst, me_head):
    requests, qcount, head_dim = grouped.shape
    per_token = qcount // DRAFT
    rows = draft_keys.shape[0]
    kv_head = me_head // 2
    own_keys = lax.dynamic_slice_in_dim(draft_keys, kv_head * head_dim, head_dim, 2)
    own_vals = lax.dynamic_slice_in_dim(draft_values, kv_head * head_dim, head_dim, 2)
    own_q = lax.dynamic_slice_in_dim(grouped, inst * rows, rows, 0)
    inv_root = 1.0 / math.sqrt(head_dim)
    scores = (
        jnp.einsum("rqd,rjd->rqj", own_q, own_keys, preferred_element_type=jnp.float32) * inv_root
    )
    causal = jnp.arange(DRAFT)[None, :] <= (jnp.arange(qcount) // per_token)[:, None]
    scores = jnp.where(causal, scores, masked)
    peaks = jnp.max(scores, axis=-1)
    weights = jnp.where(causal, jnp.exp(scores - peaks[..., None]), 0.0)
    totals = jnp.sum(weights, axis=-1)
    weighted = jnp.einsum(
        "rqj,rjd->rqd", weights.astype(jnp.bfloat16), own_vals, preferred_element_type=jnp.float32
    )
    return peaks, totals, weighted


def spread(x):
    return lax.all_to_all(x, "inst", split_axis=0, concat_axis=0, tiled=True)


def shards(old_keys, old_values, old_block, new_slot, lengths, queries, draft_keys, draft_values):
    insts = lax.axis_size("inst")
    inst = lax.axis_index("inst")
    me_head = lax.axis_index("head")
    _, entries, half, head_dim = old_keys.shape
    keys = old_keys.reshape(-1, half, head_dim)
    values = old_values.reshape(-1, half, head_dim)
    blocks = new_slot.shape[0]
    requests = queries.shape[0]
    local_heads = queries.shape[2] // head_dim
    qcount = DRAFT * local_heads
    rows = requests // insts

    out_k, out_v = pack(old_block, new_slot, keys, values)
    inbox_k = spread(out_k)
    inbox_v = spread(out_v)

    grouped = queries.reshape(requests, qcount, head_dim)
    peaks, totals, weighted = cache_partial(keys, values, old_block, lengths, grouped, me_head)
    level = jnp.where(totals > 0, peaks + jnp.log(jnp.where(totals > 0, totals, 1.0)), masked)
    mean = weighted / jnp.where(totals > 0, totals, 1.0)[..., None]
    parts = split3(level.reshape(insts, rows * qcount)).reshape(insts, -1, head_dim)
    parts = jnp.pad(parts, ((0, 0), (0, -parts.shape[1] % 16), (0, 0)))
    packet = jnp.concatenate(
        [mean.astype(jnp.bfloat16).reshape(insts, rows * qcount, head_dim), parts], axis=1
    )
    got = spread(packet)
    got_mean = got[:, : rows * qcount].reshape(insts, rows, qcount, head_dim).astype(jnp.float32)
    got_parts = got[:, rows * qcount : rows * qcount + 3 * rows * qcount // head_dim]
    got_level = jnp.sum(
        got_parts.reshape(insts, 3, rows, qcount).astype(jnp.float32), axis=1
    )
    d_peaks, d_totals, d_weighted = draft_partial(grouped, draft_keys, draft_values, inst, me_head)
    top = jnp.maximum(jnp.max(got_level, axis=0), d_peaks)
    share = jnp.exp(got_level - top[None])
    d_share = jnp.exp(d_peaks - top)
    total = jnp.sum(share, axis=0) + d_totals * d_share
    acc = jnp.sum(got_mean * share[..., None], axis=0) + d_weighted * d_share[..., None]
    mine = (acc / total[..., None]).astype(jnp.bfloat16)
    full = spread(jnp.broadcast_to(mine[None], (insts,) + mine.shape))
    attended = full.reshape(requests, DRAFT, local_heads * head_dim)

    shape = (insts, blocks // insts, entries, half, head_dim)
    moved_keys = jnp.sum(inbox_k.reshape(shape), axis=0)
    moved_values = jnp.sum(inbox_v.reshape(shape), axis=0)
    return moved_keys, moved_values, attended


def solution(mesh):
    placed = (
        P("inst", "head", None, None),
        P("inst", "head", None, None),
        P("inst"),
        P(),
        P(),
        P(None, None, "head"),
        P("inst", None, None),
        P("inst", None, None),
    )
    return jax.shard_map(
        shards,
        mesh=mesh,
        in_specs=placed,
        out_specs=(
            P("inst", "head", None, None),
            P("inst", "head", None, None),
            P(None, None, "head"),
        ),
        check_vma=False,
    )
```

time: 296 us -> 317 us (1.071)
  blocking collectives: 40 us -> 169 us
  waiting for transfers between devices: 124 us -> 67.8 us
  local copies, waits for them, and re-layouts: 51.1 us -> 11.7 us
  between operations: 14.6 us -> 1.03 us
  starting transfers between devices: 38.3 us -> 26.1 us
  matrix products: 8.53 us -> 19.1 us
  Pallas kernels: 0 us -> 3.94 us
    all_to_all x0 -> x1, blocking collectives: none -> 169 us  [spread(): return lax.all_to_all(x, 'inst', split_axis=0, concat_axis=0, tiled=True)]
    psum x1 -> x0, waiting for transfers between devices: 53.4 us -> none  [shards(): lax.psum((totals * factor, weighted * factor[..., None]), 'inst')]
    psum x1 -> x0, blocking collectives: 40 us -> none  [shards(): lax.psum((totals * factor, weighted * factor[..., None]), 'inst')]
    scatter x3 -> x0, local copies, waits for them, and re-layouts: 29.8 us -> none  [the longest x1 14.2 us: shards(): outgoing_keys = jnp.zeros((block_capacity,) + trailing_tokens, old_keys.d...]
    all_to_all x3, starting transfers between devices: 37.9 us -> 25.5 us  [spread(): return lax.all_to_all(x, 'inst', split_axis=0, concat_axis=0, tiled=True)]
    dot_general x5, matrix products: 8.28 us -> 18.8 us  [the longest x1 7.76 us: cache_partial(): jnp.einsum('sqd,std->sqt', picked, key_rows, preferred_element_type=jnp.f...]
    another operation x6 -> x2, local copies, waits for them, and re-layouts: 8.38 us -> 0.73 us  [the longest x1 0.63 us: split3(): return jnp.stack([hi, mid, low], axis=1).astype(jnp.bfloat16)]
    reduce_sum x4 -> x8, other arithmetic: 7.03 us -> 14.2 us  [the longest x1 4.65 us: cache_partial(): jnp.sum(weights, axis=-1)]
  transfers between devices with their start and end apart: 6 -> 5, of which waited for: 4 -> 3; matrix products, arithmetic and copies ran while one was open for 15% -> 11% of each run, Pallas kernels for 0% -> 1%
where the time goes in v1:
time: 317 us
  blocking collectives  169 us (53%)
  waiting for transfers between devices  67.8 us (21%)
  starting transfers between devices  26.1 us (8%)
  matrix products  19.1 us (6%)
  other arithmetic  18.5 us (6%)
  local copies, waits for them, and re-layouts  11.7 us (4%)
  Pallas kernels  3.94 us (1%)
    all_to_all x1, blocking collectives, spread(): return lax.all_to_all(x, 'inst', split_axis=0, concat_axis=0, tiled=True)  169 us
    all_to_all x3, waiting for transfers between devices, spread(): return lax.all_to_all(x, 'inst', split_axis=0, concat_axis=0, tiled=True)  67.8 us
    all_to_all x3, starting transfers between devices, spread(): return lax.all_to_all(x, 'inst', split_axis=0, concat_axis=0, tiled=True)  25.5 us
    dot_general x1, matrix products, cache_partial(): jnp.einsum('sqd,std->sqt', picked, key_rows, preferred_element_type=jnp.f...  7.76 us
  transfers between devices with their start and end apart: 5, of which 3 were waited for; matrix products, arithmetic and copies ran while one was open for 11% of the time, Pallas kernels for 1%

profile of v1, /device:TPU:0, one launch (start us, length us, event | category | flops | bytes accessed | tf_op | source)
XLA Modules:
  0.0 317.3 jit_solution(858425248243404906)
XLA Ops:
  0.6 0.0 copy-start
  0.6 0.0 copy-start.1
  0.7 0.0 copy-start.11
  0.7 0.1 collective-permute-start
  0.8 0.5 collective-permute-start.1
  1.3 0.7 fusion.58
  2.0 0.1 copy.35
  2.1 0.1 reduce-window.9
  2.2 0.1 reduce.5
  2.3 1.7 reshape.290
  4.0 0.7 fusion.57
  4.7 0.7 convert_reduce_fusion
  5.5 2.2 gather_fusion
  7.7 0.1 select_reduce_fusion.3
  7.9 0.1 fusion.28
  8.0 7.8 %fusion.10 = (f32[128,64]{1,0:T(8,128)}, f32[128,64,128]{2,1,0:T(8,128)}) fusion(pred[128,128]{1,0:T(8,128)(4,1)S(1)} %fusion.28, bf16[128,64,128]{2,1,0:T(8,128)(2,1)} %gather_fusion, bf16[128,64,128]{2,1,0:T(8,128)(2,1)} %collective-permute-done, bf16[128,64,128]{2,1,0:T(8,128)(2,1)S(1)} %bitcast.25), kind=kOutput, calls=%fused_computation.13 | convolution fusion | flops 279961600 | bytes 10534912 | tf_op jit(solution)/shard_map/sqd,std->sqt/dot_general | solution.py:109
  15.8 1.1 copy.36
  16.8 0.6 select_reduce_fusion.1
  17.5 0.6 select_reduce_fusion
  18.1 0.1 copy.37
  18.2 4.6 %fusion.11 = f32[128,64]{1,0:T(8,128)S(1)} fusion(f32[128,64,128]{2,1,0:T(8,128)} %get-tuple-element.17, f32[128,64]{1,0:T(8,128)S(1)} %copy.37, pred[128,128]{1,0:T(8,128)(4,1)S(1)} %fusion.28), kind=kLoop, calls=%fused_computation.14 | loop fusion | flops 5234688 | bytes 4276224 | tf_op jit(solution)/shard_map/reduce_sum | solution.py:119
  22.9 0.8 compare_select_fusion.1
  23.7 0.8 reshape.292
  24.6 0.6 copy.41
  25.2 0.8 convert_element_type.40
  26.0 0.7 copy.39
  26.7 3.6 %fusion.4 = f32[128,64,128]{2,1,0:T(8,128)S(1)} fusion(bf16[128,64,128]{2,1,0:T(8,128)(2,1)} %collective-permute-done.1, bf16[128,64,128]{2,1,0:T(8,128)(2,1)S(1)} %bitcast.28, f32[128,64,128]{2,1,0:T(8,128)} %get-tuple-element.17, f32[128,64]{1,0:T(8,128)S(1)} %copy.37, pred[128,128]{1,0:T(8,128)(4,1)S(1)} %fusion.28), kind=kOutput, calls=%fused_computation.5 | convolution fusion | flops 282066944 | bytes 12632064 | tf_op jit(solution)/shard_map/sqt,std->sqd/dot_general | solution.py:123
  30.3 5.7 %divide_convert_fusion = bf16[64,64,128]{2,0,1:T(8,128)(2,1)S(1)} fusion(f32[128,64,128]{2,1,0:T(8,128)S(1)} %fusion.4, f32[64,64]{0,1:T(8,128)S(1)} %copy-done.3, s32[128]{0:T(128)S(1)} %copy-done.9, pred[128]{0:T(512)(128)(4,1)S(1)} %copy-done.6), kind=kOutput, calls=%fused_computation.19 | convolution fusion | flops 806371328 | bytes 5259904 | tf_op jit(solution)/shard_map/sr,sqd->rqd/dot_general | solution.py:129
  36.0 0.7 copy.40
  36.7 1.1 fusion.26
  37.9 7.0 %all-to-all-start.2 = ((bf16[8,528,128]{2,1,0:T(8,128)(2,1)}), bf16[8,528,128]{2,1,0:T(8,128)(2,1)S(1)}, u32[]{:S(2)}, u32[]{:S(2)}) async-start(bf16[8,528,128]{2,1,0:T(8,128)(2,1)} %fusion.26), calls=%async_computation.2 | async-start | bytes 2162688 | tf_op jit(solution)/shard_map/all_to_all | solution.py:157
  44.9 3.9 %pack.1 = (bf16[256,64,128]{2,1,0:T(8,128)(2,1)}, bf16[256,64,128]{2,1,0:T(8,128)(2,1)}) custom-call(s32[128]{0:T(128)} %old_block.1, s32[256]{0:T(256)} %new_slot.1, bf16[128,64,128]{2,1,0:T(8,128)(2,1)} %bitcast.24, bf16[128,64,128]{2,1,0:T(8,128)(2,1)} %bitcast.27), custom_call_target="tpu_custom_call" | custom-call | tf_op jit(solution)/shard_map/pack/pallas_call | solution.py:64
  48.9 13.8 %all-to-all-done.2 = bf16[8,528,128]{2,1,0:T(8,128)(2,1)S(1)} async-done(((bf16[8,528,128]{2,1,0:T(8,128)(2,1)}), bf16[8,528,128]{2,1,0:T(8,128)(2,1)S(1)}, u32[]{:S(2)}, u32[]{:S(2)}) %all-to-all-start.2) | async-done | bytes 1081376 | tf_op jit(solution)/shard_map/all_to_all | solution.py:157
  62.6 169.1 %all_to_all.20 = bf16[256,64,128]{2,1,0:T(8,128)(2,1)} all-to-all(bf16[256,64,128]{2,1,0:T(8,128)(2,1)} %get-tuple-element.5), channel_id=1, replica_groups=mesh['inst'=8,'head'=16] {'inst'}, dimensions={0} | all-to-all | bytes 8388608 | tf_op jit(solution)/shard_map/all_to_all | solution.py:157
  231.7 4.7 %all-to-all-start.1 = ((bf16[256,64,128]{2,1,0:T(8,128)(2,1)}), bf16[256,64,128]{2,1,0:T(8,128)(2,1)}, u32[]{:S(2)}, u32[]{:S(2)}) async-start(bf16[256,64,128]{2,1,0:T(8,128)(2,1)} %get-tuple-element.6), calls=%async_computation.1 | async-start | bytes 8388608 | tf_op jit(solution)/shard_map/all_to_all | solution.py:157
  236.5 1.0 fusion.54
  237.6 0.1 reshape.294
  237.7 0.1 reduce_sum.113
  237.8 0.1 max.29
  237.9 0.7 multiply_reduce_fusion
  238.6 0.3 fusion.24
  238.9 47.2 %all-to-all-done.1 = bf16[256,64,128]{2,1,0:T(8,128)(2,1)} async-done(((bf16[256,64,128]{2,1,0:T(8,128)(2,1)}), bf16[256,64,128]{2,1,0:T(8,128)(2,1)}, u32[]{:S(2)}, u32[]{:S(2)}) %all-to-all-start.1) | async-done | bytes 4194336 | tf_op jit(solution)/shard_map/all_to_all | solution.py:157
  286.1 1.2 broadcast_in_dim.139
  287.3 13.7 %all-to-all-start.3 = ((bf16[8,8,64,128]{3,2,1,0:T(8,128)(2,1)}), bf16[8,8,64,128]{3,2,1,0:T(8,128)(2,1)S(1)}, u32[]{:S(2)}, u32[]{:S(2)}) async-start(bf16[8,8,64,128]{3,2,1,0:T(8,128)(2,1)} %broadcast_in_dim.139), calls=%async_computation.3 | async-start | bytes 2097152 | tf_op jit(solution)/shard_map/all_to_all | solution.py:157
  301.0 4.0 %reduce_sum.104 = bf16[32,64,128]{2,1,0:T(8,128)(2,1)} reduce(bf16[8,32,64,128]{3,2,1,0:T(8,128)(2,1)} %bitcast.21, bf16[]{:T(256)} %constant.86.clone.1), dimensions={0}, to_apply=%region_0.1 | reduce | flops 1835008 | bytes 4718594 | tf_op jit(solution)/shard_map/reduce_sum | solution.py:203
  305.0 4.0 %reduce_sum.106 = bf16[32,64,128]{2,1,0:T(8,128)(2,1)} reduce(bf16[8,32,64,128]{3,2,1,0:T(8,128)(2,1)} %bitcast.4, bf16[]{:T(256)} %constant.86.clone.1), dimensions={0}, to_apply=%region_1.2 | reduce | flops 1835008 | bytes 4718594 | tf_op jit(solution)/shard_map/reduce_sum | solution.py:204
  309.0 6.9 %all-to-all-done.3 = bf16[8,8,64,128]{3,2,1,0:T(8,128)(2,1)S(1)} async-done(((bf16[8,8,64,128]{3,2,1,0:T(8,128)(2,1)}), bf16[8,8,64,128]{3,2,1,0:T(8,128)(2,1)S(1)}, u32[]{:S(2)}, u32[]{:S(2)}) %all-to-all-start.3) | async-done | bytes 1048608 | tf_op jit(solution)/shard_map/all_to_all | solution.py:157
  315.9 1.4 reshape.293
  (42 shorter events, 0.2 us)
Async XLA Ops:
  0.6 238.0 %copy-start = (bf16[8,16,1024]{2,1,0:T(8,128)(2,1)S(1)}, bf16[8,16,1024]{2,1,0:T(8,128)(2,1)}, u32[]{:S(2)}) copy-start(bf16[8,16,1024]{2,1,0:T(8,128)(2,1)} %param.15) | copy-start | bytes 786436
  0.6 7.4 %copy-start.1 = (bf16[128,1,64,128]{3,2,1,0:T(8,128)(2,1)S(1)}, bf16[128,1,64,128]{3,2,1,0:T(8,128)(2,1)}, u32[]{:S(2)}) copy-start(bf16[128,1,64,128]{3,2,1,0:T(8,128)(2,1)} %param.8) | copy-start | bytes 6291460
  0.7 7.1 %copy-start.11 = (s32[64]{0:T(128)S(1)}, s32[64]{0:T(128)}, u32[]{:S(2)}) copy-start(s32[64]{0:T(128)} %param.12) | copy-start | bytes 772
  0.7 7.0 %copy-start.10 = (s32[128]{0:T(128)S(1)}, s32[128]{0:T(128)}, u32[]{:S(2)}) copy-start(s32[128]{0:T(128)} %old_block.1) | copy-start | bytes 1540
  0.7 7.3 %collective-permute-start = (bf16[128,64,128]{2,1,0:T(8,128)(2,1)}, bf16[128,64,128]{2,1,0:T(8,128)(2,1)}, u32[]{:S(2)}, u32[]{:S(2)}) collective-permute-start(bf16[128,64,128]{2,1,0:T(8,128)(2,1)} %bitcast.23), channel_id=1, source_target_pairs={{0,1},{1,0},{2,3},{3,2},{4,5},{5,4},{6,7},{7,6},{8,9},{9,8},{10,11... | collective-permute-start | bytes 6291464 | tf_op jit(solution)/shard_map/ppermute | solution.py:89
  0.8 25.9 %collective-permute-start.1 = (bf16[128,64,128]{2,1,0:T(8,128)(2,1)}, bf16[128,64,128]{2,1,0:T(8,128)(2,1)}, u32[]{:S(2)}, u32[]{:S(2)}) collective-permute-start(bf16[128,64,128]{2,1,0:T(8,128)(2,1)} %bitcast.26), channel_id=1, source_target_pairs={{0,1},{1,0},{2,3},{3,2},{4,5},{5,4},{6,7},{7,6},{8,9},{9,8},{10,11... | collective-permute-start | bytes 6291464 | tf_op jit(solution)/shard_map/ppermute | solution.py:90
  7.7 8.1 %copy-start.4 = (pred[128]{0:T(512)(128)(4,1)}, pred[128]{0:T(512)(128)(4,1)S(1)}, u32[]{:S(2)}) copy-start(pred[128]{0:T(512)(128)(4,1)S(1)} %broadcast_compare_fusion) | copy-start | bytes 388
  7.7 8.1 %copy-start.7 = (s32[128]{0:T(128)}, s32[128]{0:T(128)S(1)}, u32[]{:S(2)}) copy-start(s32[128]{0:T(128)S(1)} %add_clamp_fusion) | copy-start | bytes 1540
  15.8 10.9 %copy-start.2 = (bf16[128,1,64,128]{3,2,1,0:T(8,128)(2,1)S(1)}, bf16[128,1,64,128]{3,2,1,0:T(8,128)(2,1)}, u32[]{:S(2)}) copy-start(bf16[128,1,64,128]{3,2,1,0:T(8,128)(2,1)} %param.9) | copy-start | bytes 6291460
  18.2 4.7 %copy-start.5 = (pred[128]{0:T(512)(128)(4,1)S(1)}, pred[128]{0:T(512)(128)(4,1)}, u32[]{:S(2)}) copy-start(pred[128]{0:T(512)(128)(4,1)} %copy-done.4) | copy-start | bytes 388
  18.2 4.7 %copy-start.8 = (s32[128]{0:T(128)S(1)}, s32[128]{0:T(128)}, u32[]{:S(2)}) copy-start(s32[128]{0:T(128)} %copy-done.7) | copy-start | bytes 1540
  26.7 3.6 %copy-start.3 = (f32[64,64]{0,1:T(8,128)S(1)}, f32[64,64]{0,1:T(8,128)}, u32[]{:S(2)}) copy-start(f32[64,64]{0,1:T(8,128)} %copy.39) | copy-start | bytes 49156
  26.7 3.6 %copy-start.6 = (pred[128]{0:T(512)(128)(4,1)S(1)}, pred[128]{0:T(512)(128)(4,1)}, u32[]{:S(2)}) copy-start(pred[128]{0:T(512)(128)(4,1)} %copy-done.4) | copy-start | bytes 388
  26.7 3.6 %copy-start.9 = (s32[128]{0:T(128)S(1)}, s32[128]{0:T(128)}, u32[]{:S(2)}) copy-start(s32[128]{0:T(128)} %copy-done.7) | copy-start | bytes 1540
  37.9 24.8 %all-to-all-start.2 = ((bf16[8,528,128]{2,1,0:T(8,128)(2,1)}), bf16[8,528,128]{2,1,0:T(8,128)(2,1)S(1)}, u32[]{:S(2)}, u32[]{:S(2)}) async-start(bf16[8,528,128]{2,1,0:T(8,128)(2,1)} %fusion.26), calls=%async_computation.2 | async-start | bytes 2162688 | tf_op jit(solution)/shard_map/all_to_all | solution.py:157
  231.7 54.3 %all-to-all-start.1 = ((bf16[256,64,128]{2,1,0:T(8,128)(2,1)}), bf16[256,64,128]{2,1,0:T(8,128)(2,1)}, u32[]{:S(2)}, u32[]{:S(2)}) async-start(bf16[256,64,128]{2,1,0:T(8,128)(2,1)} %get-tuple-element.6), calls=%async_computation.1 | async-start | bytes 8388608 | tf_op jit(solution)/shard_map/all_to_all | solution.py:157
  287.3 28.6 %all-to-all-start.3 = ((bf16[8,8,64,128]{3,2,1,0:T(8,128)(2,1)}), bf16[8,8,64,128]{3,2,1,0:T(8,128)(2,1)S(1)}, u32[]{:S(2)}, u32[]{:S(2)}) async-start(bf16[8,8,64,128]{3,2,1,0:T(8,128)(2,1)} %broadcast_in_dim.139), calls=%async_computation.3 | async-start | bytes 2097152 | tf_op jit(solution)/shard_map/all_to_all | solution.py:157
